TPU v7x, 256 devices: a whole 4x4x8 slice. The times are simulated.
256 devices in a mesh: section: 8 (over y, x_hi), fsdp: 32 (over x_lo, z, core).
Axes of the slice: x: 4 (x_hi: 2, x_lo: 2; x = x_hi * 2 + x_lo), y: 4, z: 8, core: 2. Of those that a mesh axis runs over, the one named last changes fastest.
Arguments:
- codes: int32 [8, 8192, 512], P('section', 'fsdp'), may hold values from 0 to 15
- scale_codes: int32 [8, 8192, 8], P('section', 'fsdp'), may hold values from 0 to 255
- second_scales: float32 [8, 256], P('section', 'fsdp'), may hold values from 0.015 to 0.09
- gains: bfloat16 [8, 8192], P('section'), may hold values from 0.5 to 1.5
- down_adapter: bfloat16 [8, 8192, 64], P('section'), may hold values from -0.0625 to 0.0625
- up_projection_weight: bfloat16 [8, 512, 64], P('section'), may hold values from -0.75 to 0.75
- hidden_in: bfloat16 [4096, 8192], P('fsdp'), may hold values from -6 to 6
- cotangent: bfloat16 [4096, 8192], P('fsdp'), may hold values from -6 to 6
Outputs:
- input_grad: bfloat16 [8, 4096, 8192], P('section', 'fsdp')
- grad_down: float32 [8, 8192, 64], P('section', 'fsdp')
- grad_up: float32 [8, 512, 64], P('section', 'fsdp')
All inputs are finite; a program needn't handle non-finite values.
Results may differ from a plain program's by a relative error of at most 0.025.
Values may be sent and summed in bfloat16 or wider, within the bound.
A program may use at most 128 MiB of HBM per device.

v0:
```python
import jax
import jax.numpy as jnp
from jax import lax
from jax.sharding import PartitionSpec as P

HEAD = 128
GROUP = 8
KV_HEADS = 4
BLOCK = 64
SROWS = 32
MICRO = 4
NF4_TABLE = (
    -1.0,
    -0.6961928009986877,
    -0.5250730514526367,
    -0.39491748809814453,
    -0.28444138169288635,
    -0.18477343022823334,
    -0.09105003625154495,
    0.0,
    0.07958029955625534,
    0.16093020141124725,
    0.24611230194568634,
    0.33791524171066284,
    0.44070982933044434,
    0.5626170039176941,
    0.7229568362236023,
    1.0,
)
adapter_scale = 0.5
epsilon = 1e-05


def from_behind(block, axis, distance):
    devices = range(lax.axis_size(axis))
    route = [(i - distance, i) for i in devices if i - distance in devices]
    return lax.ppermute(block, axis, route)


def cut_along(shard, dim, length):
    lengths = shard.shape
    tiles = shard.reshape(*lengths[:dim], length, lengths[dim] // length, *lengths[dim + 1 :])
    return jnp.moveaxis(tiles, dim, 0)


def sent_and_summed(shard, axis, dim):
    tiles = cut_along(shard, dim, lax.axis_size(axis))
    arrived = lax.all_to_all(tiles, axis, split_axis=0, concat_axis=0, tiled=True)
    return arrived.astype(jnp.float32).sum(axis=0)


def dequantize_shard(codes, scale_codes, second_scales):
    value_rows = jnp.zeros(codes.shape, jnp.float32)
    for entry in range(16):
        value_rows = jnp.where(codes == entry, jnp.float32(NF4_TABLE[entry]), value_rows)
    outer = jnp.repeat(second_scales, SROWS)
    block = outer[:, None] * (scale_codes.astype(jnp.float32) + 1.0) / 256.0
    scaled = value_rows.reshape(codes.shape[0], scale_codes.shape[1], BLOCK) * block[:, :, None]
    return scaled.reshape(codes.shape).astype(jnp.bfloat16)


def spread_heads(value_rows, width):
    count = value_rows.shape[0]
    heads = value_rows.reshape(count, KV_HEADS, 1, HEAD)
    wide = jnp.broadcast_to(heads, (count, KV_HEADS, GROUP, HEAD)).reshape(
        count, KV_HEADS * GROUP * HEAD
    )
    filler = jnp.zeros((count, width - KV_HEADS * GROUP * HEAD), value_rows.dtype)
    return jnp.concatenate([wide, filler], axis=1)


def collapse_heads(grads):
    count = grads.shape[0]
    part = grads[:, : KV_HEADS * GROUP * HEAD].reshape(count, KV_HEADS, GROUP, HEAD)
    return jnp.sum(part, axis=2).reshape(count, KV_HEADS * HEAD)


def shards(
    codes,
    scale_codes,
    second_scales,
    gains,
    down_adapter,
    up_projection_weight,
    hidden_in,
    cotangent,
):
    section = lax.axis_index("section")
    sections = lax.axis_size("section")
    shard = dequantize_shard(codes[0], scale_codes[0], second_scales[0])
    weight = lax.all_gather(shard, "fsdp", axis=0, tiled=True)
    gain = gains[0].astype(jnp.float32)
    down = down_adapter[0]
    raised_output = up_projection_weight[0]
    width = hidden_in.shape[1]
    rows = hidden_in.shape[0] // MICRO
    ticks = MICRO + sections - 1
    rank = down.shape[1]
    value_width = raised_output.shape[0]

    def forward_tick(carry, tick):
        state, saved_in, saved_normed, saved_low = carry
        incoming = from_behind(state, "section", 1)
        position = tick - section
        active = (position >= 0) & (position < MICRO)
        slot = jnp.clip(position, 0, MICRO - 1)
        first = lax.dynamic_slice_in_dim(hidden_in, slot * rows, rows, 0)
        current_in = jnp.where(section == 0, first, incoming)

        def forward_compute(operands):
            current_in, saved_in, saved_normed, saved_low = operands
            current = current_in.astype(jnp.float32)
            root_mean = jnp.sqrt(jnp.mean(current * current, axis=1, keepdims=True) + epsilon)
            normalized_input = (current / root_mean * gain).astype(jnp.bfloat16)
            narrow_product = jnp.dot(
                normalized_input, down, preferred_element_type=jnp.float32
            ).astype(jnp.bfloat16)
            value_rows = jnp.dot(
                normalized_input, weight, preferred_element_type=jnp.float32
            ) + adapter_scale * jnp.dot(
                narrow_product, raised_output.T, preferred_element_type=jnp.float32
            )
            result = (current + spread_heads(value_rows, width)).astype(jnp.bfloat16)
            return (
                result,
                lax.dynamic_update_index_in_dim(saved_in, current_in, slot, 0),
                lax.dynamic_update_index_in_dim(saved_normed, normalized_input, slot, 0),
                lax.dynamic_update_index_in_dim(saved_low, narrow_product, slot, 0),
            )

        def forward_pause(operands):
            return operands

        updated = lax.cond(
            active, forward_compute, forward_pause, (current_in, saved_in, saved_normed, saved_low)
        )
        return (updated, None)

    start = (
        jnp.zeros((rows, width), jnp.bfloat16),
        jnp.zeros((MICRO, rows, width), jnp.bfloat16),
        jnp.zeros((MICRO, rows, width), jnp.bfloat16),
        jnp.zeros((MICRO, rows, rank), jnp.bfloat16),
    )
    finished, _ = lax.scan(forward_tick, start, jnp.arange(ticks, dtype=jnp.int32))
    last_state, saved_in, saved_normed, saved_low = finished

    def backward_tick(carry, tick):
        state, saved_grad, saved_direction, saved_lowgrad = carry
        incoming = from_behind(state, "section", -1)
        position = tick - (sections - 1 - section)
        active = (position >= 0) & (position < MICRO)
        slot = jnp.clip(position, 0, MICRO - 1)
        final = lax.dynamic_slice_in_dim(cotangent, slot * rows, rows, 0)
        grad_in = jnp.where(section == sections - 1, final, incoming)

        def backward_compute(operands):
            grad_in, saved_grad, saved_direction, saved_lowgrad = operands
            current = lax.dynamic_index_in_dim(saved_in, slot, 0, keepdims=False).astype(
                jnp.float32
            )
            root_mean = jnp.sqrt(jnp.mean(current * current, axis=1, keepdims=True) + epsilon)
            unit = current / root_mean
            incoming_grad = grad_in.astype(jnp.float32)
            descent_vector = collapse_heads(incoming_grad).astype(jnp.bfloat16)
            narrow_gradient = (
                adapter_scale
                * jnp.dot(descent_vector, raised_output, preferred_element_type=jnp.float32)
            ).astype(jnp.bfloat16)
            normed_grad = jnp.dot(
                descent_vector, weight.T, preferred_element_type=jnp.float32
            ) + jnp.dot(narrow_gradient, down.T, preferred_element_type=jnp.float32)
            scaled = normed_grad * gain
            hidden_grad = (
                scaled - unit * jnp.mean(scaled * unit, axis=1, keepdims=True)
            ) / root_mean
            result = (incoming_grad + hidden_grad).astype(jnp.bfloat16)
            return (
                result,
                lax.dynamic_update_index_in_dim(saved_grad, result, slot, 0),
                lax.dynamic_update_index_in_dim(saved_direction, descent_vector, slot, 0),
                lax.dynamic_update_index_in_dim(saved_lowgrad, narrow_gradient, slot, 0),
            )

        def backward_pause(operands):
            return operands

        updated = lax.cond(
            active,
            backward_compute,
            backward_pause,
            (grad_in, saved_grad, saved_direction, saved_lowgrad),
        )
        return (updated, None)

    start_back = (
        jnp.zeros((rows, width), jnp.bfloat16),
        jnp.zeros((MICRO, rows, width), jnp.bfloat16),
        jnp.zeros((MICRO, rows, value_width), jnp.bfloat16),
        jnp.zeros((MICRO, rows, rank), jnp.bfloat16),
    )
    finished_back, _ = lax.scan(backward_tick, start_back, jnp.arange(ticks, dtype=jnp.int32))
    _, saved_grad, saved_direction, saved_lowgrad = finished_back
    tokens_here = MICRO * rows
    directions = saved_direction.reshape(tokens_here, value_width)
    lowranks = saved_low.reshape(tokens_here, rank)
    normeds = saved_normed.reshape(tokens_here, width)
    low_grads = saved_lowgrad.reshape(tokens_here, rank)
    contract = (((0,), (0,)), ((), ()))
    up_weight_gradient = adapter_scale * lax.dot_general(
        directions, lowranks, contract, preferred_element_type=jnp.float32
    )
    down_grad = lax.dot_general(normeds, low_grads, contract, preferred_element_type=jnp.float32)
    down_part, up_part = (
        sent_and_summed(down_grad.astype(jnp.bfloat16), "fsdp", 0),
        sent_and_summed(up_weight_gradient.astype(jnp.bfloat16), "fsdp", 0),
    )
    input_grad = saved_grad.reshape(1, tokens_here, width)
    return (input_grad, down_part[None], up_part[None])


def solution(mesh):
    return jax.shard_map(
        shards,
        mesh=mesh,
        in_specs=(
            P("section", "fsdp", None),
            P("section", "fsdp", None),
            P("section", "fsdp"),
            P("section", None),
            P("section", None, None),
            P("section", None, None),
            P("fsdp", None),
            P("fsdp", None),
        ),
        out_specs=(
            P("section", "fsdp", None),
            P("section", "fsdp", None),
            P("section", "fsdp", None),
        ),
        check_vma=False,
    )
```

profile of v0, /device:TPU:32, one launch (start us, length us, event | category | flops | bytes accessed | tf_op | source)
XLA Modules:
  0.0 660.1 jit_solution(1380995913632222256)
XLA Ops:
  11.6 1.8 copy.52
  13.4 90.0 %all-gather.2.cloned.1.call-done = bf16[8192,512]{0,1:T(8,128)(2,1)} async-done(((bf16[256,512]{0,1:T(8,128)(2,1)}), bf16[8192,512]{0,1:T(8,128)(2,1)}) %all-gather.2.cloned.1.call-update) | async-done | bytes 8388624 | tf_op jit(solution)/shard_map/all_gather | solution.py:91
  103.4 12.0 %copy.54 = bf16[8192,512]{1,0:T(8,128)(2,1)} copy(bf16[8192,512]{0,1:T(8,128)(2,1)} %all-gather.2.cloned.1.call-done) | data formatting | bytes 16777216 | tf_op jit(solution)/shard_map/while | solution.py:202
  115.4 1.6 broadcast.190.clone.1
  117.2 215.5 %while.35 = (s32[]{:T(128)}, bf16[32,8192]{1,0:T(8,128)(2,1)S(1)}, bf16[4,32,8192]{2,1,0:T(8,128)(2,1)S(1)}, bf16[4,32,8192]{2,1,0:T(8,128)(2,1)}, bf16[4,32,64]...) while((s32[]{:T(128)}, bf16[32,8192]{1,0:T(8,128)(2,1)S(1)}, ...), condition=%wide.region_4.5_spmd, body=%wide.region_0.4_spmd.sunk | while | flops 309102624 | bytes 25221160 | solution.py:145
  117.2 4.6 collective-permute-start
  123.0 10.3 %collective-permute-done = bf16[32,8192]{1,0:T(8,128)(2,1)S(1)} collective-permute-done((bf16[32,8192]{1,0:T(8,128)(2,1)S(1)}, bf16[32,8192]{1,0:T(8,128)(2,1)S(1)}, u32[]{:S(2)}, u32[]{:S(2)}) %collective-permute-start) | collective-permute-done | bytes 524320 | tf_op jit(solution)/shard_map/while/body/eval_jaxpr/ppermute | solution.py:37
  134.5 7.7 %conditional.4 = ((bf16[32,8192]{1,0:T(8,128)(2,1)S(1)}, bf16[4,32,8192]{2,1,0:T(8,128)(2,1)S(1)}, bf16[4,32,8192]{2,1,0:T(8,128)(2,1)}, bf16[4,32,64]{2,1,0:T(8,128)(2,1)S(1)})) conditional(s32[]{:T(128)} %convert_element_type.130, (bf16[32,8192]{1,0:T(8,128)(2,1)S(1)}, bf16[4,32,8192]{2,1,0:T(8,128)(2,1)S(1)}, bf16[4,32,8192]{2,1,0:T(8,128)(2,1)}, ...), branch_computations={%region_1.1_spmd, %region_2.3_spmd} | conditional | flops 308840480 | bytes 21550702 | solution.py:134
  134.8 5.1 fusion.6
  142.2 1.3 collective-permute-start
  144.8 9.7 %collective-permute-done = bf16[32,8192]{1,0:T(8,128)(2,1)S(1)} collective-permute-done((bf16[32,8192]{1,0:T(8,128)(2,1)S(1)}, bf16[32,8192]{1,0:T(8,128)(2,1)S(1)}, u32[]{:S(2)}, u32[]{:S(2)}) %collective-permute-start) | collective-permute-done | bytes 524320 | tf_op jit(solution)/shard_map/while/body/eval_jaxpr/ppermute | solution.py:37
  155.7 7.7 %conditional.4 = ((bf16[32,8192]{1,0:T(8,128)(2,1)S(1)}, bf16[4,32,8192]{2,1,0:T(8,128)(2,1)S(1)}, bf16[4,32,8192]{2,1,0:T(8,128)(2,1)}, bf16[4,32,64]{2,1,0:T(8,128)(2,1)S(1)})) conditional(s32[]{:T(128)} %convert_element_type.130, (bf16[32,8192]{1,0:T(8,128)(2,1)S(1)}, bf16[4,32,8192]{2,1,0:T(8,128)(2,1)S(1)}, bf16[4,32,8192]{2,1,0:T(8,128)(2,1)}, ...), branch_computations={%region_1.1_spmd, %region_2.3_spmd} | conditional | flops 308840480 | bytes 21550702 | solution.py:134
  155.9 5.1 fusion.6
  163.4 5.9 collective-permute-start
  170.6 8.8 %collective-permute-done = bf16[32,8192]{1,0:T(8,128)(2,1)S(1)} collective-permute-done((bf16[32,8192]{1,0:T(8,128)(2,1)S(1)}, bf16[32,8192]{1,0:T(8,128)(2,1)S(1)}, u32[]{:S(2)}, u32[]{:S(2)}) %collective-permute-start) | collective-permute-done | bytes 524320 | tf_op jit(solution)/shard_map/while/body/eval_jaxpr/ppermute | solution.py:37
  180.6 7.7 %conditional.4 = ((bf16[32,8192]{1,0:T(8,128)(2,1)S(1)}, bf16[4,32,8192]{2,1,0:T(8,128)(2,1)S(1)}, bf16[4,32,8192]{2,1,0:T(8,128)(2,1)}, bf16[4,32,64]{2,1,0:T(8,128)(2,1)S(1)})) conditional(s32[]{:T(128)} %convert_element_type.130, (bf16[32,8192]{1,0:T(8,128)(2,1)S(1)}, bf16[4,32,8192]{2,1,0:T(8,128)(2,1)S(1)}, bf16[4,32,8192]{2,1,0:T(8,128)(2,1)}, ...), branch_computations={%region_1.1_spmd, %region_2.3_spmd} | conditional | flops 308840480 | bytes 21550702 | solution.py:134
  180.9 5.1 fusion.6
  188.3 6.0 collective-permute-start
  195.5 8.0 %collective-permute-done = bf16[32,8192]{1,0:T(8,128)(2,1)S(1)} collective-permute-done((bf16[32,8192]{1,0:T(8,128)(2,1)S(1)}, bf16[32,8192]{1,0:T(8,128)(2,1)S(1)}, u32[]{:S(2)}, u32[]{:S(2)}) %collective-permute-start) | collective-permute-done | bytes 524320 | tf_op jit(solution)/shard_map/while/body/eval_jaxpr/ppermute | solution.py:37
  204.7 7.7 %conditional.4 = ((bf16[32,8192]{1,0:T(8,128)(2,1)S(1)}, bf16[4,32,8192]{2,1,0:T(8,128)(2,1)S(1)}, bf16[4,32,8192]{2,1,0:T(8,128)(2,1)}, bf16[4,32,64]{2,1,0:T(8,128)(2,1)S(1)})) conditional(s32[]{:T(128)} %convert_element_type.130, (bf16[32,8192]{1,0:T(8,128)(2,1)S(1)}, bf16[4,32,8192]{2,1,0:T(8,128)(2,1)S(1)}, bf16[4,32,8192]{2,1,0:T(8,128)(2,1)}, ...), branch_computations={%region_1.1_spmd, %region_2.3_spmd} | conditional | flops 308840480 | bytes 21550702 | solution.py:134
  204.9 5.1 fusion.6
  212.3 5.9 collective-permute-start
  219.5 7.1 %collective-permute-done = bf16[32,8192]{1,0:T(8,128)(2,1)S(1)} collective-permute-done((bf16[32,8192]{1,0:T(8,128)(2,1)S(1)}, bf16[32,8192]{1,0:T(8,128)(2,1)S(1)}, u32[]{:S(2)}, u32[]{:S(2)}) %collective-permute-start) | collective-permute-done | bytes 524320 | tf_op jit(solution)/shard_map/while/body/eval_jaxpr/ppermute | solution.py:37
  227.9 13.6 %collective-permute-start = (bf16[32,8192]{1,0:T(8,128)(2,1)S(1)}, bf16[32,8192]{1,0:T(8,128)(2,1)S(1)}, u32[]{:S(2)}, u32[]{:S(2)}) collective-permute-start(bf16[32,8192]{1,0:T(8,128)(2,1)S(1)} %get-tuple-element.701), channel_id=1, source_target_pairs={{0,32},{32,64},{64,96},{96,128},{128,160},{160,192},{192,224},{1,3... | collective-permute-start | bytes 1572872 | tf_op jit(solution)/shard_map/while/body/eval_jaxpr/ppermute | solution.py:37
  242.7 6.3 collective-permute-done
  250.2 5.9 collective-permute-start
  257.3 5.6 collective-permute-done
  264.2 14.5 %collective-permute-start = (bf16[32,8192]{1,0:T(8,128)(2,1)S(1)}, bf16[32,8192]{1,0:T(8,128)(2,1)S(1)}, u32[]{:S(2)}, u32[]{:S(2)}) collective-permute-start(bf16[32,8192]{1,0:T(8,128)(2,1)S(1)} %get-tuple-element.701), channel_id=1, source_target_pairs={{0,32},{32,64},{64,96},{96,128},{128,160},{160,192},{192,224},{1,3... | collective-permute-start | bytes 1572872 | tf_op jit(solution)/shard_map/while/body/eval_jaxpr/ppermute | solution.py:37
  279.9 5.4 collective-permute-done
  286.5 6.8 %collective-permute-start = (bf16[32,8192]{1,0:T(8,128)(2,1)S(1)}, bf16[32,8192]{1,0:T(8,128)(2,1)S(1)}, u32[]{:S(2)}, u32[]{:S(2)}) collective-permute-start(bf16[32,8192]{1,0:T(8,128)(2,1)S(1)} %get-tuple-element.701), channel_id=1, source_target_pairs={{0,32},{32,64},{64,96},{96,128},{128,160},{160,192},{192,224},{1,3... | collective-permute-start | bytes 1572872 | tf_op jit(solution)/shard_map/while/body/eval_jaxpr/ppermute | solution.py:37
  294.6 5.4 collective-permute-done
  301.2 9.0 %collective-permute-start = (bf16[32,8192]{1,0:T(8,128)(2,1)S(1)}, bf16[32,8192]{1,0:T(8,128)(2,1)S(1)}, u32[]{:S(2)}, u32[]{:S(2)}) collective-permute-start(bf16[32,8192]{1,0:T(8,128)(2,1)S(1)} %get-tuple-element.701), channel_id=1, source_target_pairs={{0,32},{32,64},{64,96},{96,128},{128,160},{160,192},{192,224},{1,3... | collective-permute-start | bytes 1572872 | tf_op jit(solution)/shard_map/while/body/eval_jaxpr/ppermute | solution.py:37
  311.4 5.4 collective-permute-done
  318.0 6.8 %collective-permute-start = (bf16[32,8192]{1,0:T(8,128)(2,1)S(1)}, bf16[32,8192]{1,0:T(8,128)(2,1)S(1)}, u32[]{:S(2)}, u32[]{:S(2)}) collective-permute-start(bf16[32,8192]{1,0:T(8,128)(2,1)S(1)} %get-tuple-element.701), channel_id=1, source_target_pairs={{0,32},{32,64},{64,96},{96,128},{128,160},{160,192},{192,224},{1,3... | collective-permute-start | bytes 1572872 | tf_op jit(solution)/shard_map/while/body/eval_jaxpr/ppermute | solution.py:37
  326.1 5.4 collective-permute-done
  332.8 1.5 broadcast.190
  334.3 271.0 %while.36 = (s32[]{:T(128)}, bf16[32,8192]{1,0:T(8,128)(2,1)S(1)}, bf16[4,32,8192]{2,1,0:T(8,128)(2,1)}, bf16[4,32,512]{2,1,0:T(8,128)(2,1)S(1)}, bf16[4,32,64]{...) while((s32[]{:T(128)}, bf16[32,8192]{1,0:T(8,128)(2,1)S(1)}, ...), condition=%wide.region_11.12_spmd, body=%wide.region_5.11_spmd.sunk | while | flops 309186592 | bytes 28268232 | solution.py:202
  336.8 19.6 %collective-permute-done.1 = bf16[32,8192]{1,0:T(8,128)(2,1)S(1)} collective-permute-done((bf16[32,8192]{1,0:T(8,128)(2,1)S(1)}, bf16[32,8192]{1,0:T(8,128)(2,1)S(1)}, u32[]{:S(2)}, u32[]{:S(2)}) %collective-permute-start.1) | collective-permute-done | bytes 524320 | tf_op jit(solution)/shard_map/while/body/eval_jaxpr/ppermute | solution.py:37
  357.6 1.3 collective-permute-start.1
  360.2 11.3 %collective-permute-done.1 = bf16[32,8192]{1,0:T(8,128)(2,1)S(1)} collective-permute-done((bf16[32,8192]{1,0:T(8,128)(2,1)S(1)}, bf16[32,8192]{1,0:T(8,128)(2,1)S(1)}, u32[]{:S(2)}, u32[]{:S(2)}) %collective-permute-start.1) | collective-permute-done | bytes 524320 | tf_op jit(solution)/shard_map/while/body/eval_jaxpr/ppermute | solution.py:37
  372.7 1.3 collective-permute-start.1
  375.3 22.6 %collective-permute-done.1 = bf16[32,8192]{1,0:T(8,128)(2,1)S(1)} collective-permute-done((bf16[32,8192]{1,0:T(8,128)(2,1)S(1)}, bf16[32,8192]{1,0:T(8,128)(2,1)S(1)}, u32[]{:S(2)}, u32[]{:S(2)}) %collective-permute-start.1) | collective-permute-done | bytes 524320 | tf_op jit(solution)/shard_map/while/body/eval_jaxpr/ppermute | solution.py:37
  399.0 1.3 collective-permute-start.1
  401.6 14.8 %collective-permute-done.1 = bf16[32,8192]{1,0:T(8,128)(2,1)S(1)} collective-permute-done((bf16[32,8192]{1,0:T(8,128)(2,1)S(1)}, bf16[32,8192]{1,0:T(8,128)(2,1)S(1)}, u32[]{:S(2)}, u32[]{:S(2)}) %collective-permute-start.1) | collective-permute-done | bytes 524320 | tf_op jit(solution)/shard_map/while/body/eval_jaxpr/ppermute | solution.py:37
  420.1 19.9 %collective-permute-done.1 = bf16[32,8192]{1,0:T(8,128)(2,1)S(1)} collective-permute-done((bf16[32,8192]{1,0:T(8,128)(2,1)S(1)}, bf16[32,8192]{1,0:T(8,128)(2,1)S(1)}, u32[]{:S(2)}, u32[]{:S(2)}) %collective-permute-start.1) | collective-permute-done | bytes 524320 | tf_op jit(solution)/shard_map/while/body/eval_jaxpr/ppermute | solution.py:37
  443.8 17.1 %collective-permute-done.1 = bf16[32,8192]{1,0:T(8,128)(2,1)S(1)} collective-permute-done((bf16[32,8192]{1,0:T(8,128)(2,1)S(1)}, bf16[32,8192]{1,0:T(8,128)(2,1)S(1)}, u32[]{:S(2)}, u32[]{:S(2)}) %collective-permute-start.1) | collective-permute-done | bytes 524320 | tf_op jit(solution)/shard_map/while/body/eval_jaxpr/ppermute | solution.py:37
  464.7 10.0 %collective-permute-done.1 = bf16[32,8192]{1,0:T(8,128)(2,1)S(1)} collective-permute-done((bf16[32,8192]{1,0:T(8,128)(2,1)S(1)}, bf16[32,8192]{1,0:T(8,128)(2,1)S(1)}, u32[]{:S(2)}, u32[]{:S(2)}) %collective-permute-start.1) | collective-permute-done | bytes 524320 | tf_op jit(solution)/shard_map/while/body/eval_jaxpr/ppermute | solution.py:37
  478.5 43.8 %collective-permute-done.1 = bf16[32,8192]{1,0:T(8,128)(2,1)S(1)} collective-permute-done((bf16[32,8192]{1,0:T(8,128)(2,1)S(1)}, bf16[32,8192]{1,0:T(8,128)(2,1)S(1)}, u32[]{:S(2)}, u32[]{:S(2)}) %collective-permute-start.1) | collective-permute-done | bytes 524320 | tf_op jit(solution)/shard_map/while/body/eval_jaxpr/ppermute | solution.py:37
  523.5 8.8 %conditional.5 = ((bf16[32,8192]{1,0:T(8,128)(2,1)S(1)}, bf16[4,32,8192]{2,1,0:T(8,128)(2,1)}, bf16[4,32,512]{2,1,0:T(8,128)(2,1)S(1)}, bf16[4,32,64]{2,1,0:T(8,128)(2,1)S(1)})) conditional(s32[]{:T(128)} %convert_element_type.131, (bf16[32,8192]{1,0:T(8,128)(2,1)S(1)}, bf16[4,32,8192]{2,1,0:T(8,128)(2,1)}, bf16[4,32,512]{2,1,0:T(8,128)(2,1)S(1)}, ...), branch_computations={%region_6.6_spmd, %region_7.10_spmd} | conditional | flops 308924448 | bytes 24597758 | solution.py:188
  523.9 6.1 fusion.12
  534.9 10.9 %collective-permute-done.1 = bf16[32,8192]{1,0:T(8,128)(2,1)S(1)} collective-permute-done((bf16[32,8192]{1,0:T(8,128)(2,1)S(1)}, bf16[32,8192]{1,0:T(8,128)(2,1)S(1)}, u32[]{:S(2)}, u32[]{:S(2)}) %collective-permute-start.1) | collective-permute-done | bytes 524320 | tf_op jit(solution)/shard_map/while/body/eval_jaxpr/ppermute | solution.py:37
  547.0 8.8 %conditional.5 = ((bf16[32,8192]{1,0:T(8,128)(2,1)S(1)}, bf16[4,32,8192]{2,1,0:T(8,128)(2,1)}, bf16[4,32,512]{2,1,0:T(8,128)(2,1)S(1)}, bf16[4,32,64]{2,1,0:T(8,128)(2,1)S(1)})) conditional(s32[]{:T(128)} %convert_element_type.131, (bf16[32,8192]{1,0:T(8,128)(2,1)S(1)}, bf16[4,32,8192]{2,1,0:T(8,128)(2,1)}, bf16[4,32,512]{2,1,0:T(8,128)(2,1)S(1)}, ...), branch_computations={%region_6.6_spmd, %region_7.10_spmd} | conditional | flops 308924448 | bytes 24597758 | solution.py:188
  547.4 6.1 fusion.12
  558.3 11.5 %collective-permute-done.1 = bf16[32,8192]{1,0:T(8,128)(2,1)S(1)} collective-permute-done((bf16[32,8192]{1,0:T(8,128)(2,1)S(1)}, bf16[32,8192]{1,0:T(8,128)(2,1)S(1)}, u32[]{:S(2)}, u32[]{:S(2)}) %collective-permute-start.1) | collective-permute-done | bytes 524320 | tf_op jit(solution)/shard_map/while/body/eval_jaxpr/ppermute | solution.py:37
  571.0 8.8 %conditional.5 = ((bf16[32,8192]{1,0:T(8,128)(2,1)S(1)}, bf16[4,32,8192]{2,1,0:T(8,128)(2,1)}, bf16[4,32,512]{2,1,0:T(8,128)(2,1)S(1)}, bf16[4,32,64]{2,1,0:T(8,128)(2,1)S(1)})) conditional(s32[]{:T(128)} %convert_element_type.131, (bf16[32,8192]{1,0:T(8,128)(2,1)S(1)}, bf16[4,32,8192]{2,1,0:T(8,128)(2,1)}, bf16[4,32,512]{2,1,0:T(8,128)(2,1)S(1)}, ...), branch_computations={%region_6.6_spmd, %region_7.10_spmd} | conditional | flops 308924448 | bytes 24597758 | solution.py:188
  571.4 6.1 fusion.12
  582.4 12.9 %collective-permute-done.1 = bf16[32,8192]{1,0:T(8,128)(2,1)S(1)} collective-permute-done((bf16[32,8192]{1,0:T(8,128)(2,1)S(1)}, bf16[32,8192]{1,0:T(8,128)(2,1)S(1)}, u32[]{:S(2)}, u32[]{:S(2)}) %collective-permute-start.1) | collective-permute-done | bytes 524320 | tf_op jit(solution)/shard_map/while/body/eval_jaxpr/ppermute | solution.py:37
  596.4 8.8 %conditional.5 = ((bf16[32,8192]{1,0:T(8,128)(2,1)S(1)}, bf16[4,32,8192]{2,1,0:T(8,128)(2,1)}, bf16[4,32,512]{2,1,0:T(8,128)(2,1)S(1)}, bf16[4,32,64]{2,1,0:T(8,128)(2,1)S(1)})) conditional(s32[]{:T(128)} %convert_element_type.131, (bf16[32,8192]{1,0:T(8,128)(2,1)S(1)}, bf16[4,32,8192]{2,1,0:T(8,128)(2,1)}, bf16[4,32,512]{2,1,0:T(8,128)(2,1)S(1)}, ...), branch_computations={%region_6.6_spmd, %region_7.10_spmd} | conditional | flops 308924448 | bytes 24597758 | solution.py:188
  596.9 6.1 fusion.12
  606.4 4.2 all-to-all-start.1
  610.5 2.1 fusion.16
  613.7 4.7 all-to-all-done.1
  618.4 5.0 all-to-all-start
  624.2 28.3 %all-to-all-done = bf16[32,256,64]{1,2,0:T(8,128)(2,1)S(1)} async-done(((bf16[32,256,64]{1,2,0:T(8,128)(2,1)}), bf16[32,256,64]{1,2,0:T(8,128)(2,1)S(1)}, u32[]{:S(2)}, u32[]{:S(2)}) %all-to-all-start) | async-done | bytes 1048608 | tf_op jit(solution)/shard_map/all_to_all | solution.py:48
  (196 shorter events, 78.1 us)
Async XLA Ops:
  7.2 4.2 copy-start.4
  7.2 4.3 copy-start.3
  7.2 4.4 copy-start.2
  7.2 96.2 %all-gather.2.cloned.1.call-start = ((), (), s32[]{:S(2)}) async-start(), calls=%async_computation.2 | async-start | bytes 8650752 | tf_op jit(solution)/shard_map/all_gather | solution.py:91
  117.2 16.1 %collective-permute-start = (bf16[32,8192]{1,0:T(8,128)(2,1)S(1)}, bf16[32,8192]{1,0:T(8,128)(2,1)S(1)}, u32[]{:S(2)}, u32[]{:S(2)}) collective-permute-start(bf16[32,8192]{1,0:T(8,128)(2,1)S(1)} %get-tuple-element.701), channel_id=1, source_target_pairs={{0,32},{32,64},{64,96},{96,128},{128,160},{160,192},{192,224},{1,3... | collective-permute-start | bytes 1572872 | tf_op jit(solution)/shard_map/while/body/eval_jaxpr/ppermute | solution.py:37
  134.7 5.1 copy-start
  142.2 12.3 %collective-permute-start = (bf16[32,8192]{1,0:T(8,128)(2,1)S(1)}, bf16[32,8192]{1,0:T(8,128)(2,1)S(1)}, u32[]{:S(2)}, u32[]{:S(2)}) collective-permute-start(bf16[32,8192]{1,0:T(8,128)(2,1)S(1)} %get-tuple-element.701), channel_id=1, source_target_pairs={{0,32},{32,64},{64,96},{96,128},{128,160},{160,192},{192,224},{1,3... | collective-permute-start | bytes 1572872 | tf_op jit(solution)/shard_map/while/body/eval_jaxpr/ppermute | solution.py:37
  155.9 5.1 copy-start
  163.4 16.0 %collective-permute-start = (bf16[32,8192]{1,0:T(8,128)(2,1)S(1)}, bf16[32,8192]{1,0:T(8,128)(2,1)S(1)}, u32[]{:S(2)}, u32[]{:S(2)}) collective-permute-start(bf16[32,8192]{1,0:T(8,128)(2,1)S(1)} %get-tuple-element.701), channel_id=1, source_target_pairs={{0,32},{32,64},{64,96},{96,128},{128,160},{160,192},{192,224},{1,3... | collective-permute-start | bytes 1572872 | tf_op jit(solution)/shard_map/while/body/eval_jaxpr/ppermute | solution.py:37
  180.9 5.1 copy-start
  188.3 15.2 %collective-permute-start = (bf16[32,8192]{1,0:T(8,128)(2,1)S(1)}, bf16[32,8192]{1,0:T(8,128)(2,1)S(1)}, u32[]{:S(2)}, u32[]{:S(2)}) collective-permute-start(bf16[32,8192]{1,0:T(8,128)(2,1)S(1)} %get-tuple-element.701), channel_id=1, source_target_pairs={{0,32},{32,64},{64,96},{96,128},{128,160},{160,192},{192,224},{1,3... | collective-permute-start | bytes 1572872 | tf_op jit(solution)/shard_map/while/body/eval_jaxpr/ppermute | solution.py:37
  204.9 5.1 copy-start
  212.3 14.3 %collective-permute-start = (bf16[32,8192]{1,0:T(8,128)(2,1)S(1)}, bf16[32,8192]{1,0:T(8,128)(2,1)S(1)}, u32[]{:S(2)}, u32[]{:S(2)}) collective-permute-start(bf16[32,8192]{1,0:T(8,128)(2,1)S(1)} %get-tuple-element.701), channel_id=1, source_target_pairs={{0,32},{32,64},{64,96},{96,128},{128,160},{160,192},{192,224},{1,3... | collective-permute-start | bytes 1572872 | tf_op jit(solution)/shard_map/while/body/eval_jaxpr/ppermute | solution.py:37
  227.9 21.1 %collective-permute-start = (bf16[32,8192]{1,0:T(8,128)(2,1)S(1)}, bf16[32,8192]{1,0:T(8,128)(2,1)S(1)}, u32[]{:S(2)}, u32[]{:S(2)}) collective-permute-start(bf16[32,8192]{1,0:T(8,128)(2,1)S(1)} %get-tuple-element.701), channel_id=1, source_target_pairs={{0,32},{32,64},{64,96},{96,128},{128,160},{160,192},{192,224},{1,3... | collective-permute-start | bytes 1572872 | tf_op jit(solution)/shard_map/while/body/eval_jaxpr/ppermute | solution.py:37
  250.2 12.8 %collective-permute-start = (bf16[32,8192]{1,0:T(8,128)(2,1)S(1)}, bf16[32,8192]{1,0:T(8,128)(2,1)S(1)}, u32[]{:S(2)}, u32[]{:S(2)}) collective-permute-start(bf16[32,8192]{1,0:T(8,128)(2,1)S(1)} %get-tuple-element.701), channel_id=1, source_target_pairs={{0,32},{32,64},{64,96},{96,128},{128,160},{160,192},{192,224},{1,3... | collective-permute-start | bytes 1572872 | tf_op jit(solution)/shard_map/while/body/eval_jaxpr/ppermute | solution.py:37
  264.2 21.1 %collective-permute-start = (bf16[32,8192]{1,0:T(8,128)(2,1)S(1)}, bf16[32,8192]{1,0:T(8,128)(2,1)S(1)}, u32[]{:S(2)}, u32[]{:S(2)}) collective-permute-start(bf16[32,8192]{1,0:T(8,128)(2,1)S(1)} %get-tuple-element.701), channel_id=1, source_target_pairs={{0,32},{32,64},{64,96},{96,128},{128,160},{160,192},{192,224},{1,3... | collective-permute-start | bytes 1572872 | tf_op jit(solution)/shard_map/while/body/eval_jaxpr/ppermute | solution.py:37
  286.5 13.5 %collective-permute-start = (bf16[32,8192]{1,0:T(8,128)(2,1)S(1)}, bf16[32,8192]{1,0:T(8,128)(2,1)S(1)}, u32[]{:S(2)}, u32[]{:S(2)}) collective-permute-start(bf16[32,8192]{1,0:T(8,128)(2,1)S(1)} %get-tuple-element.701), channel_id=1, source_target_pairs={{0,32},{32,64},{64,96},{96,128},{128,160},{160,192},{192,224},{1,3... | collective-permute-start | bytes 1572872 | tf_op jit(solution)/shard_map/while/body/eval_jaxpr/ppermute | solution.py:37
  301.2 15.6 %collective-permute-start = (bf16[32,8192]{1,0:T(8,128)(2,1)S(1)}, bf16[32,8192]{1,0:T(8,128)(2,1)S(1)}, u32[]{:S(2)}, u32[]{:S(2)}) collective-permute-start(bf16[32,8192]{1,0:T(8,128)(2,1)S(1)} %get-tuple-element.701), channel_id=1, source_target_pairs={{0,32},{32,64},{64,96},{96,128},{128,160},{160,192},{192,224},{1,3... | collective-permute-start | bytes 1572872 | tf_op jit(solution)/shard_map/while/body/eval_jaxpr/ppermute | solution.py:37
  318.0 13.5 %collective-permute-start = (bf16[32,8192]{1,0:T(8,128)(2,1)S(1)}, bf16[32,8192]{1,0:T(8,128)(2,1)S(1)}, u32[]{:S(2)}, u32[]{:S(2)}) collective-permute-start(bf16[32,8192]{1,0:T(8,128)(2,1)S(1)} %get-tuple-element.701), channel_id=1, source_target_pairs={{0,32},{32,64},{64,96},{96,128},{128,160},{160,192},{192,224},{1,3... | collective-permute-start | bytes 1572872 | tf_op jit(solution)/shard_map/while/body/eval_jaxpr/ppermute | solution.py:37
  334.3 22.1 %collective-permute-start.1 = (bf16[32,8192]{1,0:T(8,128)(2,1)S(1)}, bf16[32,8192]{1,0:T(8,128)(2,1)S(1)}, u32[]{:S(2)}, u32[]{:S(2)}) collective-permute-start(bf16[32,8192]{1,0:T(8,128)(2,1)S(1)} %get-tuple-element.759), channel_id=1, source_target_pairs={{32,0},{64,32},{96,64},{128,96},{160,128},{192,160},{224,192},{33,... | collective-permute-start | bytes 1572872 | tf_op jit(solution)/shard_map/while/body/eval_jaxpr/ppermute | solution.py:37
  357.6 13.9 %collective-permute-start.1 = (bf16[32,8192]{1,0:T(8,128)(2,1)S(1)}, bf16[32,8192]{1,0:T(8,128)(2,1)S(1)}, u32[]{:S(2)}, u32[]{:S(2)}) collective-permute-start(bf16[32,8192]{1,0:T(8,128)(2,1)S(1)} %get-tuple-element.759), channel_id=1, source_target_pairs={{32,0},{64,32},{96,64},{128,96},{160,128},{192,160},{224,192},{33,... | collective-permute-start | bytes 1572872 | tf_op jit(solution)/shard_map/while/body/eval_jaxpr/ppermute | solution.py:37
  372.7 25.1 %collective-permute-start.1 = (bf16[32,8192]{1,0:T(8,128)(2,1)S(1)}, bf16[32,8192]{1,0:T(8,128)(2,1)S(1)}, u32[]{:S(2)}, u32[]{:S(2)}) collective-permute-start(bf16[32,8192]{1,0:T(8,128)(2,1)S(1)} %get-tuple-element.759), channel_id=1, source_target_pairs={{32,0},{64,32},{96,64},{128,96},{160,128},{192,160},{224,192},{33,... | collective-permute-start | bytes 1572872 | tf_op jit(solution)/shard_map/while/body/eval_jaxpr/ppermute | solution.py:37
  399.0 17.3 %collective-permute-start.1 = (bf16[32,8192]{1,0:T(8,128)(2,1)S(1)}, bf16[32,8192]{1,0:T(8,128)(2,1)S(1)}, u32[]{:S(2)}, u32[]{:S(2)}) collective-permute-start(bf16[32,8192]{1,0:T(8,128)(2,1)S(1)} %get-tuple-element.759), channel_id=1, source_target_pairs={{32,0},{64,32},{96,64},{128,96},{160,128},{192,160},{224,192},{33,... | collective-permute-start | bytes 1572872 | tf_op jit(solution)/shard_map/while/body/eval_jaxpr/ppermute | solution.py:37
  417.6 22.5 %collective-permute-start.1 = (bf16[32,8192]{1,0:T(8,128)(2,1)S(1)}, bf16[32,8192]{1,0:T(8,128)(2,1)S(1)}, u32[]{:S(2)}, u32[]{:S(2)}) collective-permute-start(bf16[32,8192]{1,0:T(8,128)(2,1)S(1)} %get-tuple-element.759), channel_id=1, source_target_pairs={{32,0},{64,32},{96,64},{128,96},{160,128},{192,160},{224,192},{33,... | collective-permute-start | bytes 1572872 | tf_op jit(solution)/shard_map/while/body/eval_jaxpr/ppermute | solution.py:37
  441.3 19.6 %collective-permute-start.1 = (bf16[32,8192]{1,0:T(8,128)(2,1)S(1)}, bf16[32,8192]{1,0:T(8,128)(2,1)S(1)}, u32[]{:S(2)}, u32[]{:S(2)}) collective-permute-start(bf16[32,8192]{1,0:T(8,128)(2,1)S(1)} %get-tuple-element.759), channel_id=1, source_target_pairs={{32,0},{64,32},{96,64},{128,96},{160,128},{192,160},{224,192},{33,... | collective-permute-start | bytes 1572872 | tf_op jit(solution)/shard_map/while/body/eval_jaxpr/ppermute | solution.py:37
  462.1 12.6 %collective-permute-start.1 = (bf16[32,8192]{1,0:T(8,128)(2,1)S(1)}, bf16[32,8192]{1,0:T(8,128)(2,1)S(1)}, u32[]{:S(2)}, u32[]{:S(2)}) collective-permute-start(bf16[32,8192]{1,0:T(8,128)(2,1)S(1)} %get-tuple-element.759), channel_id=1, source_target_pairs={{32,0},{64,32},{96,64},{128,96},{160,128},{192,160},{224,192},{33,... | collective-permute-start | bytes 1572872 | tf_op jit(solution)/shard_map/while/body/eval_jaxpr/ppermute | solution.py:37
  475.9 46.4 %collective-permute-start.1 = (bf16[32,8192]{1,0:T(8,128)(2,1)S(1)}, bf16[32,8192]{1,0:T(8,128)(2,1)S(1)}, u32[]{:S(2)}, u32[]{:S(2)}) collective-permute-start(bf16[32,8192]{1,0:T(8,128)(2,1)S(1)} %get-tuple-element.759), channel_id=1, source_target_pairs={{32,0},{64,32},{96,64},{128,96},{160,128},{192,160},{224,192},{33,... | collective-permute-start | bytes 1572872 | tf_op jit(solution)/shard_map/while/body/eval_jaxpr/ppermute | solution.py:37
  523.9 6.2 copy-start.1
  532.3 13.5 %collective-permute-start.1 = (bf16[32,8192]{1,0:T(8,128)(2,1)S(1)}, bf16[32,8192]{1,0:T(8,128)(2,1)S(1)}, u32[]{:S(2)}, u32[]{:S(2)}) collective-permute-start(bf16[32,8192]{1,0:T(8,128)(2,1)S(1)} %get-tuple-element.759), channel_id=1, source_target_pairs={{32,0},{64,32},{96,64},{128,96},{160,128},{192,160},{224,192},{33,... | collective-permute-start | bytes 1572872 | tf_op jit(solution)/shard_map/while/body/eval_jaxpr/ppermute | solution.py:37
  547.4 6.2 copy-start.1
  555.8 14.0 %collective-permute-start.1 = (bf16[32,8192]{1,0:T(8,128)(2,1)S(1)}, bf16[32,8192]{1,0:T(8,128)(2,1)S(1)}, u32[]{:S(2)}, u32[]{:S(2)}) collective-permute-start(bf16[32,8192]{1,0:T(8,128)(2,1)S(1)} %get-tuple-element.759), channel_id=1, source_target_pairs={{32,0},{64,32},{96,64},{128,96},{160,128},{192,160},{224,192},{33,... | collective-permute-start | bytes 1572872 | tf_op jit(solution)/shard_map/while/body/eval_jaxpr/ppermute | solution.py:37
  571.4 6.2 copy-start.1
  579.8 15.5 %collective-permute-start.1 = (bf16[32,8192]{1,0:T(8,128)(2,1)S(1)}, bf16[32,8192]{1,0:T(8,128)(2,1)S(1)}, u32[]{:S(2)}, u32[]{:S(2)}) collective-permute-start(bf16[32,8192]{1,0:T(8,128)(2,1)S(1)} %get-tuple-element.759), channel_id=1, source_target_pairs={{32,0},{64,32},{96,64},{128,96},{160,128},{192,160},{224,192},{33,... | collective-permute-start | bytes 1572872 | tf_op jit(solution)/shard_map/while/body/eval_jaxpr/ppermute | solution.py:37
  596.9 6.2 copy-start.1
  606.4 12.1 %all-to-all-start.1 = ((bf16[32,2,512]{2,1,0:T(2,128)(2,1)}), bf16[32,2,512]{2,1,0:T(2,128)(2,1)S(1)}, u32[]{:S(2)}, u32[]{:S(2)}) async-start(bf16[32,2,512]{2,1,0:T(2,128)(2,1)} %reshape.170), calls=%async_computation.1 | async-start | bytes 131072 | tf_op jit(solution)/shard_map/all_to_all | solution.py:48
  618.4 34.1 %all-to-all-start = ((bf16[32,256,64]{1,2,0:T(8,128)(2,1)}), bf16[32,256,64]{1,2,0:T(8,128)(2,1)S(1)}, u32[]{:S(2)}, u32[]{:S(2)}) async-start(bf16[32,256,64]{1,2,0:T(8,128)(2,1)} %bitcast.84), calls=%async_computation | async-start | bytes 2097152 | tf_op jit(solution)/shard_map/all_to_all | solution.py:48
Sparse Core Ops, SparseCore 0:
  11.5 91.8 all-gather.1
where the time goes:
time: 663 us; the launch traced here: 660 us
  waiting for transfers between devices  395 us (60%)
  starting transfers between devices  104 us (16%)
  matrix products  54 us (8%)
  other arithmetic  40.8 us (6%)
  local copies, waits for them, and re-layouts  36.4 us (5%)
  loops' own time  16.3 us (2%)
  between operations  14.2 us (2%)
    ppermute x22, waiting for transfers between devices, from_behind(): return lax.ppermute(block, axis, route)  272 us
    ppermute x22, starting transfers between devices, from_behind(): return lax.ppermute(block, axis, route)  94.5 us
    all_gather x1, waiting for transfers between devices, shards(): weight = lax.all_gather(shard, 'fsdp', axis=0, tiled=True)  90 us
    all_to_all x2, waiting for transfers between devices, sent_and_summed(): lax.all_to_all(tiles, axis, split_axis=0, concat_axis=0, tiled=True)  33 us
    dot_general x4, matrix products, backward_compute(): jnp.dot(descent_vector, weight.T, preferred_element_type=jnp.float32)  24.2 us
    dot_general x4, matrix products, forward_compute(): jnp.dot(normalized_input, weight, preferred_element_type=jnp.float32)  20.5 us
  transfers between devices with their start and end apart: 25, of which 25 were waited for; matrix products, arithmetic and copies ran while one was open for 3% of the time, Pallas kernels for 0%

commit v1 on v0

--- a/solution.py
+++ b/solution.py
@@ -88,7 +88,9 @@
     section = lax.axis_index("section")
     sections = lax.axis_size("section")
     shard = dequantize_shard(codes[0], scale_codes[0], second_scales[0])
-    weight = lax.all_gather(shard, "fsdp", axis=0, tiled=True)
+    weight = jnp.concatenate(
+        lax.all_to_all(jnp.stack([shard] * lax.axis_size("fsdp")), "fsdp", 0, 0), axis=0
+    )
     gain = gains[0].astype(jnp.float32)
     down = down_adapter[0]
     raised_output = up_projection_weight[0]

time: 663 us -> 761 us (1.15)
  waiting for transfers between devices: 395 us -> 488 us
  starting transfers between devices: 104 us -> 124 us
  between operations: 14.2 us -> 0.81 us
    all_to_all x0 -> x1, waiting for transfers between devices: none -> 181 us  [shards(): lax.all_to_all(jnp.stack([shard] * lax.axis_size('fsdp')), 'fsdp', 0, 0)]
    all_gather x1 -> x0, waiting for transfers between devices: 90 us -> none  [shards(): weight = lax.all_gather(shard, 'fsdp', axis=0, tiled=True)]
    while x1 -> x0, local copies, waits for them, and re-layouts: 12 us -> none  [shards(): lax.scan(backward_tick, start_back, jnp.arange(ticks, dtype=jnp.int32))]
    all_to_all x0 -> x1, starting transfers between devices: none -> 9.84 us  [shards(): lax.all_to_all(jnp.stack([shard] * lax.axis_size('fsdp')), 'fsdp', 0, 0)]
where the time goes in v1:
time: 761 us; the launch traced here: 759 us
  waiting for transfers between devices  488 us (64%)
  starting transfers between devices  124 us (16%)
  matrix products  59.7 us (8%)
  other arithmetic  40 us (5%)
  local copies, waits for them, and re-layouts  29.5 us (4%)
  loops' own time  16.7 us (2%)
    ppermute x22, waiting for transfers between devices, from_behind(): return lax.ppermute(block, axis, route)  274 us
    all_to_all x1, waiting for transfers between devices, shards(): lax.all_to_all(jnp.stack([shard] * lax.axis_size('fsdp')), 'fsdp', 0, 0)  181 us
    ppermute x22, starting transfers between devices, from_behind(): return lax.ppermute(block, axis, route)  99.5 us
    all_to_all x2, waiting for transfers between devices, sent_and_summed(): lax.all_to_all(tiles, axis, split_axis=0, concat_axis=0, tiled=True)  33.1 us
    dot_general x4, matrix products, backward_compute(): jnp.dot(descent_vector, weight.T, preferred_element_type=jnp.float32)  24.2 us
    dot_general x4, matrix products, forward_compute(): jnp.dot(normalized_input, weight, preferred_element_type=jnp.float32)  19.9 us
  transfers between devices with their start and end apart: 25, of which 25 were waited for; matrix products, arithmetic and copies ran while one was open for 3% of the time, Pallas kernels for 0%

profile of v1, /device:TPU:32, one launch (start us, length us, event | category | flops | bytes accessed | tf_op | source)
XLA Modules:
  0.0 758.7 jit_solution(12123168122989946652)
XLA Ops:
  4.1 4.2 stack.5
  8.3 9.8 %all-to-all-start = ((bf16[32,256,512]{2,1,0:T(8,128)(2,1)}), bf16[32,256,512]{2,1,0:T(8,128)(2,1)}, u32[]{:S(2)}, u32[]{:S(2)}) async-start(bf16[32,256,512]{2,1,0:T(8,128)(2,1)} %stack.5), calls=%async_computation | async-start | bytes 16777216 | tf_op jit(solution)/shard_map/all_to_all | solution.py:92
  18.2 1.8 copy.52
  20.2 181.0 %all-to-all-done = bf16[32,256,512]{2,1,0:T(8,128)(2,1)} async-done(((bf16[32,256,512]{2,1,0:T(8,128)(2,1)}), bf16[32,256,512]{2,1,0:T(8,128)(2,1)}, u32[]{:S(2)}, u32[]{:S(2)}) %all-to-all-start) | async-done | bytes 8388640 | tf_op jit(solution)/shard_map/all_to_all | solution.py:92
  201.4 1.6 broadcast.184.clone.1
  203.0 220.7 %while.35 = (s32[]{:T(128)}, bf16[32,8192]{1,0:T(8,128)(2,1)S(1)}, bf16[4,32,8192]{2,1,0:T(8,128)(2,1)S(1)}, bf16[4,32,8192]{2,1,0:T(8,128)(2,1)}, bf16[4,32,64]...) while((s32[]{:T(128)}, bf16[32,8192]{1,0:T(8,128)(2,1)S(1)}, ...), condition=%wide.region_4.5_spmd, body=%wide.region_0.4_spmd.sunk | while | flops 309102624 | bytes 19978252 | solution.py:147
  203.0 4.7 collective-permute-start
  209.0 8.8 %collective-permute-done = bf16[32,8192]{1,0:T(8,128)(2,1)S(1)} collective-permute-done((bf16[32,8192]{1,0:T(8,128)(2,1)S(1)}, bf16[32,8192]{1,0:T(8,128)(2,1)S(1)}, u32[]{:S(2)}, u32[]{:S(2)}) %collective-permute-start) | collective-permute-done | bytes 524320 | tf_op jit(solution)/shard_map/while/body/eval_jaxpr/ppermute | solution.py:37
  219.0 9.1 %conditional.4 = ((bf16[32,8192]{1,0:T(8,128)(2,1)S(1)}, bf16[4,32,8192]{2,1,0:T(8,128)(2,1)S(1)}, bf16[4,32,8192]{2,1,0:T(8,128)(2,1)}, bf16[4,32,64]{2,1,0:T(8,128)(2,1)S(1)})) conditional(s32[]{:T(128)} %convert_element_type.131, (bf16[32,8192]{1,0:T(8,128)(2,1)S(1)}, bf16[4,32,8192]{2,1,0:T(8,128)(2,1)S(1)}, bf16[4,32,8192]{2,1,0:T(8,128)(2,1)}, ...), branch_computations={%region_1.1_spmd, %region_2.3_spmd} | conditional | flops 308840480 | bytes 16307794 | solution.py:136
  219.3 2.1 bitcast_dynamic-update-slice_fusion.2
  221.4 5.0 fusion.6
  230.9 8.3 %collective-permute-done = bf16[32,8192]{1,0:T(8,128)(2,1)S(1)} collective-permute-done((bf16[32,8192]{1,0:T(8,128)(2,1)S(1)}, bf16[32,8192]{1,0:T(8,128)(2,1)S(1)}, u32[]{:S(2)}, u32[]{:S(2)}) %collective-permute-start) | collective-permute-done | bytes 524320 | tf_op jit(solution)/shard_map/while/body/eval_jaxpr/ppermute | solution.py:37
  240.3 9.1 %conditional.4 = ((bf16[32,8192]{1,0:T(8,128)(2,1)S(1)}, bf16[4,32,8192]{2,1,0:T(8,128)(2,1)S(1)}, bf16[4,32,8192]{2,1,0:T(8,128)(2,1)}, bf16[4,32,64]{2,1,0:T(8,128)(2,1)S(1)})) conditional(s32[]{:T(128)} %convert_element_type.131, (bf16[32,8192]{1,0:T(8,128)(2,1)S(1)}, bf16[4,32,8192]{2,1,0:T(8,128)(2,1)S(1)}, bf16[4,32,8192]{2,1,0:T(8,128)(2,1)}, ...), branch_computations={%region_1.1_spmd, %region_2.3_spmd} | conditional | flops 308840480 | bytes 16307794 | solution.py:136
  240.6 2.1 bitcast_dynamic-update-slice_fusion.2
  242.6 5.0 fusion.6
  249.4 5.9 collective-permute-start
  256.7 7.4 collective-permute-done
  265.3 9.1 %conditional.4 = ((bf16[32,8192]{1,0:T(8,128)(2,1)S(1)}, bf16[4,32,8192]{2,1,0:T(8,128)(2,1)S(1)}, bf16[4,32,8192]{2,1,0:T(8,128)(2,1)}, bf16[4,32,64]{2,1,0:T(8,128)(2,1)S(1)})) conditional(s32[]{:T(128)} %convert_element_type.131, (bf16[32,8192]{1,0:T(8,128)(2,1)S(1)}, bf16[4,32,8192]{2,1,0:T(8,128)(2,1)S(1)}, bf16[4,32,8192]{2,1,0:T(8,128)(2,1)}, ...), branch_computations={%region_1.1_spmd, %region_2.3_spmd} | conditional | flops 308840480 | bytes 16307794 | solution.py:136
  265.6 2.1 bitcast_dynamic-update-slice_fusion.2
  267.6 5.0 fusion.6
  274.4 6.0 collective-permute-start
  281.7 6.5 collective-permute-done
  289.4 9.1 %conditional.4 = ((bf16[32,8192]{1,0:T(8,128)(2,1)S(1)}, bf16[4,32,8192]{2,1,0:T(8,128)(2,1)S(1)}, bf16[4,32,8192]{2,1,0:T(8,128)(2,1)}, bf16[4,32,64]{2,1,0:T(8,128)(2,1)S(1)})) conditional(s32[]{:T(128)} %convert_element_type.131, (bf16[32,8192]{1,0:T(8,128)(2,1)S(1)}, bf16[4,32,8192]{2,1,0:T(8,128)(2,1)S(1)}, bf16[4,32,8192]{2,1,0:T(8,128)(2,1)}, ...), branch_computations={%region_1.1_spmd, %region_2.3_spmd} | conditional | flops 308840480 | bytes 16307794 | solution.py:136
  289.7 2.1 bitcast_dynamic-update-slice_fusion.2
  291.8 5.0 fusion.6
  298.5 5.9 collective-permute-start
  305.8 5.7 collective-permute-done
  312.7 15.0 %collective-permute-start = (bf16[32,8192]{1,0:T(8,128)(2,1)S(1)}, bf16[32,8192]{1,0:T(8,128)(2,1)S(1)}, u32[]{:S(2)}, u32[]{:S(2)}) collective-permute-start(bf16[32,8192]{1,0:T(8,128)(2,1)S(1)} %get-tuple-element.647), channel_id=1, source_target_pairs={{0,32},{32,64},{64,96},{96,128},{128,160},{160,192},{192,224},{1,3... | collective-permute-start | bytes 1572872 | tf_op jit(solution)/shard_map/while/body/eval_jaxpr/ppermute | solution.py:37
  329.1 5.3 collective-permute-done
  335.5 5.9 collective-permute-start
  342.8 5.3 collective-permute-done
  349.3 15.5 %collective-permute-start = (bf16[32,8192]{1,0:T(8,128)(2,1)S(1)}, bf16[32,8192]{1,0:T(8,128)(2,1)S(1)}, u32[]{:S(2)}, u32[]{:S(2)}) collective-permute-start(bf16[32,8192]{1,0:T(8,128)(2,1)S(1)} %get-tuple-element.647), channel_id=1, source_target_pairs={{0,32},{32,64},{64,96},{96,128},{128,160},{160,192},{192,224},{1,3... | collective-permute-start | bytes 1572872 | tf_op jit(solution)/shard_map/while/body/eval_jaxpr/ppermute | solution.py:37
  366.2 5.3 collective-permute-done
  372.7 6.8 collective-permute-start
  380.9 5.3 collective-permute-done
  387.4 12.4 %collective-permute-start = (bf16[32,8192]{1,0:T(8,128)(2,1)S(1)}, bf16[32,8192]{1,0:T(8,128)(2,1)S(1)}, u32[]{:S(2)}, u32[]{:S(2)}) collective-permute-start(bf16[32,8192]{1,0:T(8,128)(2,1)S(1)} %get-tuple-element.647), channel_id=1, source_target_pairs={{0,32},{32,64},{64,96},{96,128},{128,160},{160,192},{192,224},{1,3... | collective-permute-start | bytes 1572872 | tf_op jit(solution)/shard_map/while/body/eval_jaxpr/ppermute | solution.py:37
  401.1 7.6 %collective-permute-done = bf16[32,8192]{1,0:T(8,128)(2,1)S(1)} collective-permute-done((bf16[32,8192]{1,0:T(8,128)(2,1)S(1)}, bf16[32,8192]{1,0:T(8,128)(2,1)S(1)}, u32[]{:S(2)}, u32[]{:S(2)}) %collective-permute-start) | collective-permute-done | bytes 524320 | tf_op jit(solution)/shard_map/while/body/eval_jaxpr/ppermute | solution.py:37
  409.9 5.9 collective-permute-start
  417.2 5.3 collective-permute-done
  425.3 279.7 %while.36 = (s32[]{:T(128)}, bf16[32,8192]{1,0:T(8,128)(2,1)S(1)}, bf16[4,32,8192]{2,1,0:T(8,128)(2,1)}, bf16[4,32,512]{2,1,0:T(8,128)(2,1)S(1)}, bf16[4,32,64]{...) while((s32[]{:T(128)}, bf16[32,8192]{1,0:T(8,128)(2,1)S(1)}, ...), condition=%wide.region_11.12_spmd, body=%wide.region_5.11_spmd.sunk | while | flops 309186592 | bytes 28268232 | solution.py:204
  427.9 22.3 %collective-permute-done.1 = bf16[32,8192]{1,0:T(8,128)(2,1)S(1)} collective-permute-done((bf16[32,8192]{1,0:T(8,128)(2,1)S(1)}, bf16[32,8192]{1,0:T(8,128)(2,1)S(1)}, u32[]{:S(2)}, u32[]{:S(2)}) %collective-permute-start.1) | collective-permute-done | bytes 524320 | tf_op jit(solution)/shard_map/while/body/eval_jaxpr/ppermute | solution.py:37
  453.9 12.2 %collective-permute-done.1 = bf16[32,8192]{1,0:T(8,128)(2,1)S(1)} collective-permute-done((bf16[32,8192]{1,0:T(8,128)(2,1)S(1)}, bf16[32,8192]{1,0:T(8,128)(2,1)S(1)}, u32[]{:S(2)}, u32[]{:S(2)}) %collective-permute-start.1) | collective-permute-done | bytes 524320 | tf_op jit(solution)/shard_map/while/body/eval_jaxpr/ppermute | solution.py:37
  469.9 20.3 %collective-permute-done.1 = bf16[32,8192]{1,0:T(8,128)(2,1)S(1)} collective-permute-done((bf16[32,8192]{1,0:T(8,128)(2,1)S(1)}, bf16[32,8192]{1,0:T(8,128)(2,1)S(1)}, u32[]{:S(2)}, u32[]{:S(2)}) %collective-permute-start.1) | collective-permute-done | bytes 524320 | tf_op jit(solution)/shard_map/while/body/eval_jaxpr/ppermute | solution.py:37
  494.0 16.3 %collective-permute-done.1 = bf16[32,8192]{1,0:T(8,128)(2,1)S(1)} collective-permute-done((bf16[32,8192]{1,0:T(8,128)(2,1)S(1)}, bf16[32,8192]{1,0:T(8,128)(2,1)S(1)}, u32[]{:S(2)}, u32[]{:S(2)}) %collective-permute-start.1) | collective-permute-done | bytes 524320 | tf_op jit(solution)/shard_map/while/body/eval_jaxpr/ppermute | solution.py:37
  514.1 22.8 %collective-permute-done.1 = bf16[32,8192]{1,0:T(8,128)(2,1)S(1)} collective-permute-done((bf16[32,8192]{1,0:T(8,128)(2,1)S(1)}, bf16[32,8192]{1,0:T(8,128)(2,1)S(1)}, u32[]{:S(2)}, u32[]{:S(2)}) %collective-permute-start.1) | collective-permute-done | bytes 524320 | tf_op jit(solution)/shard_map/while/body/eval_jaxpr/ppermute | solution.py:37
  540.6 15.7 %collective-permute-done.1 = bf16[32,8192]{1,0:T(8,128)(2,1)S(1)} collective-permute-done((bf16[32,8192]{1,0:T(8,128)(2,1)S(1)}, bf16[32,8192]{1,0:T(8,128)(2,1)S(1)}, u32[]{:S(2)}, u32[]{:S(2)}) %collective-permute-start.1) | collective-permute-done | bytes 524320 | tf_op jit(solution)/shard_map/while/body/eval_jaxpr/ppermute | solution.py:37
  560.1 10.0 %collective-permute-done.1 = bf16[32,8192]{1,0:T(8,128)(2,1)S(1)} collective-permute-done((bf16[32,8192]{1,0:T(8,128)(2,1)S(1)}, bf16[32,8192]{1,0:T(8,128)(2,1)S(1)}, u32[]{:S(2)}, u32[]{:S(2)}) %collective-permute-start.1) | collective-permute-done | bytes 524320 | tf_op jit(solution)/shard_map/while/body/eval_jaxpr/ppermute | solution.py:37
  573.9 40.0 %collective-permute-done.1 = bf16[32,8192]{1,0:T(8,128)(2,1)S(1)} collective-permute-done((bf16[32,8192]{1,0:T(8,128)(2,1)S(1)}, bf16[32,8192]{1,0:T(8,128)(2,1)S(1)}, u32[]{:S(2)}, u32[]{:S(2)}) %collective-permute-start.1) | collective-permute-done | bytes 524320 | tf_op jit(solution)/shard_map/while/body/eval_jaxpr/ppermute | solution.py:37
  615.1 8.8 %conditional.5 = ((bf16[32,8192]{1,0:T(8,128)(2,1)S(1)}, bf16[4,32,8192]{2,1,0:T(8,128)(2,1)}, bf16[4,32,512]{2,1,0:T(8,128)(2,1)S(1)}, bf16[4,32,64]{2,1,0:T(8,128)(2,1)S(1)})) conditional(s32[]{:T(128)} %convert_element_type.132, (bf16[32,8192]{1,0:T(8,128)(2,1)S(1)}, bf16[4,32,8192]{2,1,0:T(8,128)(2,1)}, bf16[4,32,512]{2,1,0:T(8,128)(2,1)S(1)}, ...), branch_computations={%region_6.6_spmd, %region_7.10_spmd} | conditional | flops 308924448 | bytes 24597758 | solution.py:190
  615.7 6.1 fusion.12
  626.5 12.4 %collective-permute-done.1 = bf16[32,8192]{1,0:T(8,128)(2,1)S(1)} collective-permute-done((bf16[32,8192]{1,0:T(8,128)(2,1)S(1)}, bf16[32,8192]{1,0:T(8,128)(2,1)S(1)}, u32[]{:S(2)}, u32[]{:S(2)}) %collective-permute-start.1) | collective-permute-done | bytes 524320 | tf_op jit(solution)/shard_map/while/body/eval_jaxpr/ppermute | solution.py:37
  640.1 8.8 %conditional.5 = ((bf16[32,8192]{1,0:T(8,128)(2,1)S(1)}, bf16[4,32,8192]{2,1,0:T(8,128)(2,1)}, bf16[4,32,512]{2,1,0:T(8,128)(2,1)S(1)}, bf16[4,32,64]{2,1,0:T(8,128)(2,1)S(1)})) conditional(s32[]{:T(128)} %convert_element_type.132, (bf16[32,8192]{1,0:T(8,128)(2,1)S(1)}, bf16[4,32,8192]{2,1,0:T(8,128)(2,1)}, bf16[4,32,512]{2,1,0:T(8,128)(2,1)S(1)}, ...), branch_computations={%region_6.6_spmd, %region_7.10_spmd} | conditional | flops 308924448 | bytes 24597758 | solution.py:190
  640.7 6.1 fusion.12
  651.5 13.8 %collective-permute-done.1 = bf16[32,8192]{1,0:T(8,128)(2,1)S(1)} collective-permute-done((bf16[32,8192]{1,0:T(8,128)(2,1)S(1)}, bf16[32,8192]{1,0:T(8,128)(2,1)S(1)}, u32[]{:S(2)}, u32[]{:S(2)}) %collective-permute-start.1) | collective-permute-done | bytes 524320 | tf_op jit(solution)/shard_map/while/body/eval_jaxpr/ppermute | solution.py:37
  666.5 8.8 %conditional.5 = ((bf16[32,8192]{1,0:T(8,128)(2,1)S(1)}, bf16[4,32,8192]{2,1,0:T(8,128)(2,1)}, bf16[4,32,512]{2,1,0:T(8,128)(2,1)S(1)}, bf16[4,32,64]{2,1,0:T(8,128)(2,1)S(1)})) conditional(s32[]{:T(128)} %convert_element_type.132, (bf16[32,8192]{1,0:T(8,128)(2,1)S(1)}, bf16[4,32,8192]{2,1,0:T(8,128)(2,1)}, bf16[4,32,512]{2,1,0:T(8,128)(2,1)S(1)}, ...), branch_computations={%region_6.6_spmd, %region_7.10_spmd} | conditional | flops 308924448 | bytes 24597758 | solution.py:190
  667.1 6.1 fusion.12
  677.9 17.2 %collective-permute-done.1 = bf16[32,8192]{1,0:T(8,128)(2,1)S(1)} collective-permute-done((bf16[32,8192]{1,0:T(8,128)(2,1)S(1)}, bf16[32,8192]{1,0:T(8,128)(2,1)S(1)}, u32[]{:S(2)}, u32[]{:S(2)}) %collective-permute-start.1) | collective-permute-done | bytes 524320 | tf_op jit(solution)/shard_map/while/body/eval_jaxpr/ppermute | solution.py:37
  696.2 8.8 %conditional.5 = ((bf16[32,8192]{1,0:T(8,128)(2,1)S(1)}, bf16[4,32,8192]{2,1,0:T(8,128)(2,1)}, bf16[4,32,512]{2,1,0:T(8,128)(2,1)S(1)}, bf16[4,32,64]{2,1,0:T(8,128)(2,1)S(1)})) conditional(s32[]{:T(128)} %convert_element_type.132, (bf16[32,8192]{1,0:T(8,128)(2,1)S(1)}, bf16[4,32,8192]{2,1,0:T(8,128)(2,1)}, bf16[4,32,512]{2,1,0:T(8,128)(2,1)S(1)}, ...), branch_computations={%region_6.6_spmd, %region_7.10_spmd} | conditional | flops 308924448 | bytes 24597758 | solution.py:190
  696.8 6.1 fusion.12
  706.1 9.7 %all-to-all-start.2 = ((bf16[32,2,512]{2,1,0:T(2,128)(2,1)}), bf16[32,2,512]{2,1,0:T(2,128)(2,1)S(1)}, u32[]{:S(2)}, u32[]{:S(2)}) async-start(bf16[32,2,512]{2,1,0:T(2,128)(2,1)} %reshape.113), calls=%async_computation.2 | async-start | bytes 131072 | tf_op jit(solution)/shard_map/all_to_all | solution.py:48
  715.9 2.1 fusion.16
  719.1 4.8 all-to-all-done.2
  723.9 5.0 all-to-all-start.1
  729.7 28.3 %all-to-all-done.1 = bf16[32,256,64]{1,2,0:T(8,128)(2,1)S(1)} async-done(((bf16[32,256,64]{1,2,0:T(8,128)(2,1)}), bf16[32,256,64]{1,2,0:T(8,128)(2,1)S(1)}, u32[]{:S(2)}, u32[]{:S(2)}) %all-to-all-start.1) | async-done | bytes 1048608 | tf_op jit(solution)/shard_map/all_to_all | solution.py:48
  (188 shorter events, 82.9 us)
Async XLA Ops:
  8.3 9.9 %copy-start.1 = (bf16[1,8192,64]{1,2,0:T(8,128)(2,1)S(1)}, bf16[1,8192,64]{1,2,0:T(8,128)(2,1)}, u32[]{:S(2)}) copy-start(bf16[1,8192,64]{1,2,0:T(8,128)(2,1)} %param.20) | copy-start | bytes 3145732
  8.3 192.9 %all-to-all-start = ((bf16[32,256,512]{2,1,0:T(8,128)(2,1)}), bf16[32,256,512]{2,1,0:T(8,128)(2,1)}, u32[]{:S(2)}, u32[]{:S(2)}) async-start(bf16[32,256,512]{2,1,0:T(8,128)(2,1)} %stack.5), calls=%async_computation | async-start | bytes 16777216 | tf_op jit(solution)/shard_map/all_to_all | solution.py:92
  18.1 1.9 copy-start.2
  18.1 2.0 copy-start.3
  203.0 14.9 %collective-permute-start = (bf16[32,8192]{1,0:T(8,128)(2,1)S(1)}, bf16[32,8192]{1,0:T(8,128)(2,1)S(1)}, u32[]{:S(2)}, u32[]{:S(2)}) collective-permute-start(bf16[32,8192]{1,0:T(8,128)(2,1)S(1)} %get-tuple-element.647), channel_id=1, source_target_pairs={{0,32},{32,64},{64,96},{96,128},{128,160},{160,192},{192,224},{1,3... | collective-permute-start | bytes 1572872 | tf_op jit(solution)/shard_map/while/body/eval_jaxpr/ppermute | solution.py:37
  228.2 11.0 %collective-permute-start = (bf16[32,8192]{1,0:T(8,128)(2,1)S(1)}, bf16[32,8192]{1,0:T(8,128)(2,1)S(1)}, u32[]{:S(2)}, u32[]{:S(2)}) collective-permute-start(bf16[32,8192]{1,0:T(8,128)(2,1)S(1)} %get-tuple-element.647), channel_id=1, source_target_pairs={{0,32},{32,64},{64,96},{96,128},{128,160},{160,192},{192,224},{1,3... | collective-permute-start | bytes 1572872 | tf_op jit(solution)/shard_map/while/body/eval_jaxpr/ppermute | solution.py:37
  249.4 14.7 %collective-permute-start = (bf16[32,8192]{1,0:T(8,128)(2,1)S(1)}, bf16[32,8192]{1,0:T(8,128)(2,1)S(1)}, u32[]{:S(2)}, u32[]{:S(2)}) collective-permute-start(bf16[32,8192]{1,0:T(8,128)(2,1)S(1)} %get-tuple-element.647), channel_id=1, source_target_pairs={{0,32},{32,64},{64,96},{96,128},{128,160},{160,192},{192,224},{1,3... | collective-permute-start | bytes 1572872 | tf_op jit(solution)/shard_map/while/body/eval_jaxpr/ppermute | solution.py:37
  274.4 13.9 %collective-permute-start = (bf16[32,8192]{1,0:T(8,128)(2,1)S(1)}, bf16[32,8192]{1,0:T(8,128)(2,1)S(1)}, u32[]{:S(2)}, u32[]{:S(2)}) collective-permute-start(bf16[32,8192]{1,0:T(8,128)(2,1)S(1)} %get-tuple-element.647), channel_id=1, source_target_pairs={{0,32},{32,64},{64,96},{96,128},{128,160},{160,192},{192,224},{1,3... | collective-permute-start | bytes 1572872 | tf_op jit(solution)/shard_map/while/body/eval_jaxpr/ppermute | solution.py:37
  298.5 13.0 %collective-permute-start = (bf16[32,8192]{1,0:T(8,128)(2,1)S(1)}, bf16[32,8192]{1,0:T(8,128)(2,1)S(1)}, u32[]{:S(2)}, u32[]{:S(2)}) collective-permute-start(bf16[32,8192]{1,0:T(8,128)(2,1)S(1)} %get-tuple-element.647), channel_id=1, source_target_pairs={{0,32},{32,64},{64,96},{96,128},{128,160},{160,192},{192,224},{1,3... | collective-permute-start | bytes 1572872 | tf_op jit(solution)/shard_map/while/body/eval_jaxpr/ppermute | solution.py:37
  312.7 21.6 %collective-permute-start = (bf16[32,8192]{1,0:T(8,128)(2,1)S(1)}, bf16[32,8192]{1,0:T(8,128)(2,1)S(1)}, u32[]{:S(2)}, u32[]{:S(2)}) collective-permute-start(bf16[32,8192]{1,0:T(8,128)(2,1)S(1)} %get-tuple-element.647), channel_id=1, source_target_pairs={{0,32},{32,64},{64,96},{96,128},{128,160},{160,192},{192,224},{1,3... | collective-permute-start | bytes 1572872 | tf_op jit(solution)/shard_map/while/body/eval_jaxpr/ppermute | solution.py:37
  335.5 12.6 %collective-permute-start = (bf16[32,8192]{1,0:T(8,128)(2,1)S(1)}, bf16[32,8192]{1,0:T(8,128)(2,1)S(1)}, u32[]{:S(2)}, u32[]{:S(2)}) collective-permute-start(bf16[32,8192]{1,0:T(8,128)(2,1)S(1)} %get-tuple-element.647), channel_id=1, source_target_pairs={{0,32},{32,64},{64,96},{96,128},{128,160},{160,192},{192,224},{1,3... | collective-permute-start | bytes 1572872 | tf_op jit(solution)/shard_map/while/body/eval_jaxpr/ppermute | solution.py:37
  349.3 22.1 %collective-permute-start = (bf16[32,8192]{1,0:T(8,128)(2,1)S(1)}, bf16[32,8192]{1,0:T(8,128)(2,1)S(1)}, u32[]{:S(2)}, u32[]{:S(2)}) collective-permute-start(bf16[32,8192]{1,0:T(8,128)(2,1)S(1)} %get-tuple-element.647), channel_id=1, source_target_pairs={{0,32},{32,64},{64,96},{96,128},{128,160},{160,192},{192,224},{1,3... | collective-permute-start | bytes 1572872 | tf_op jit(solution)/shard_map/while/body/eval_jaxpr/ppermute | solution.py:37
  372.7 13.5 %collective-permute-start = (bf16[32,8192]{1,0:T(8,128)(2,1)S(1)}, bf16[32,8192]{1,0:T(8,128)(2,1)S(1)}, u32[]{:S(2)}, u32[]{:S(2)}) collective-permute-start(bf16[32,8192]{1,0:T(8,128)(2,1)S(1)} %get-tuple-element.647), channel_id=1, source_target_pairs={{0,32},{32,64},{64,96},{96,128},{128,160},{160,192},{192,224},{1,3... | collective-permute-start | bytes 1572872 | tf_op jit(solution)/shard_map/while/body/eval_jaxpr/ppermute | solution.py:37
  387.4 21.4 %collective-permute-start = (bf16[32,8192]{1,0:T(8,128)(2,1)S(1)}, bf16[32,8192]{1,0:T(8,128)(2,1)S(1)}, u32[]{:S(2)}, u32[]{:S(2)}) collective-permute-start(bf16[32,8192]{1,0:T(8,128)(2,1)S(1)} %get-tuple-element.647), channel_id=1, source_target_pairs={{0,32},{32,64},{64,96},{96,128},{128,160},{160,192},{192,224},{1,3... | collective-permute-start | bytes 1572872 | tf_op jit(solution)/shard_map/while/body/eval_jaxpr/ppermute | solution.py:37
  409.9 12.6 %collective-permute-start = (bf16[32,8192]{1,0:T(8,128)(2,1)S(1)}, bf16[32,8192]{1,0:T(8,128)(2,1)S(1)}, u32[]{:S(2)}, u32[]{:S(2)}) collective-permute-start(bf16[32,8192]{1,0:T(8,128)(2,1)S(1)} %get-tuple-element.647), channel_id=1, source_target_pairs={{0,32},{32,64},{64,96},{96,128},{128,160},{160,192},{192,224},{1,3... | collective-permute-start | bytes 1572872 | tf_op jit(solution)/shard_map/while/body/eval_jaxpr/ppermute | solution.py:37
  425.3 24.8 %collective-permute-start.1 = (bf16[32,8192]{1,0:T(8,128)(2,1)S(1)}, bf16[32,8192]{1,0:T(8,128)(2,1)S(1)}, u32[]{:S(2)}, u32[]{:S(2)}) collective-permute-start(bf16[32,8192]{1,0:T(8,128)(2,1)S(1)} %get-tuple-element.705), channel_id=1, source_target_pairs={{32,0},{64,32},{96,64},{128,96},{160,128},{192,160},{224,192},{33,... | collective-permute-start | bytes 1572872 | tf_op jit(solution)/shard_map/while/body/eval_jaxpr/ppermute | solution.py:37
  451.4 14.8 %collective-permute-start.1 = (bf16[32,8192]{1,0:T(8,128)(2,1)S(1)}, bf16[32,8192]{1,0:T(8,128)(2,1)S(1)}, u32[]{:S(2)}, u32[]{:S(2)}) collective-permute-start(bf16[32,8192]{1,0:T(8,128)(2,1)S(1)} %get-tuple-element.705), channel_id=1, source_target_pairs={{32,0},{64,32},{96,64},{128,96},{160,128},{192,160},{224,192},{33,... | collective-permute-start | bytes 1572872 | tf_op jit(solution)/shard_map/while/body/eval_jaxpr/ppermute | solution.py:37
  467.4 22.9 %collective-permute-start.1 = (bf16[32,8192]{1,0:T(8,128)(2,1)S(1)}, bf16[32,8192]{1,0:T(8,128)(2,1)S(1)}, u32[]{:S(2)}, u32[]{:S(2)}) collective-permute-start(bf16[32,8192]{1,0:T(8,128)(2,1)S(1)} %get-tuple-element.705), channel_id=1, source_target_pairs={{32,0},{64,32},{96,64},{128,96},{160,128},{192,160},{224,192},{33,... | collective-permute-start | bytes 1572872 | tf_op jit(solution)/shard_map/while/body/eval_jaxpr/ppermute | solution.py:37
  491.4 18.8 %collective-permute-start.1 = (bf16[32,8192]{1,0:T(8,128)(2,1)S(1)}, bf16[32,8192]{1,0:T(8,128)(2,1)S(1)}, u32[]{:S(2)}, u32[]{:S(2)}) collective-permute-start(bf16[32,8192]{1,0:T(8,128)(2,1)S(1)} %get-tuple-element.705), channel_id=1, source_target_pairs={{32,0},{64,32},{96,64},{128,96},{160,128},{192,160},{224,192},{33,... | collective-permute-start | bytes 1572872 | tf_op jit(solution)/shard_map/while/body/eval_jaxpr/ppermute | solution.py:37
  511.5 25.3 %collective-permute-start.1 = (bf16[32,8192]{1,0:T(8,128)(2,1)S(1)}, bf16[32,8192]{1,0:T(8,128)(2,1)S(1)}, u32[]{:S(2)}, u32[]{:S(2)}) collective-permute-start(bf16[32,8192]{1,0:T(8,128)(2,1)S(1)} %get-tuple-element.705), channel_id=1, source_target_pairs={{32,0},{64,32},{96,64},{128,96},{160,128},{192,160},{224,192},{33,... | collective-permute-start | bytes 1572872 | tf_op jit(solution)/shard_map/while/body/eval_jaxpr/ppermute | solution.py:37
  538.0 18.3 %collective-permute-start.1 = (bf16[32,8192]{1,0:T(8,128)(2,1)S(1)}, bf16[32,8192]{1,0:T(8,128)(2,1)S(1)}, u32[]{:S(2)}, u32[]{:S(2)}) collective-permute-start(bf16[32,8192]{1,0:T(8,128)(2,1)S(1)} %get-tuple-element.705), channel_id=1, source_target_pairs={{32,0},{64,32},{96,64},{128,96},{160,128},{192,160},{224,192},{33,... | collective-permute-start | bytes 1572872 | tf_op jit(solution)/shard_map/while/body/eval_jaxpr/ppermute | solution.py:37
  557.5 12.6 %collective-permute-start.1 = (bf16[32,8192]{1,0:T(8,128)(2,1)S(1)}, bf16[32,8192]{1,0:T(8,128)(2,1)S(1)}, u32[]{:S(2)}, u32[]{:S(2)}) collective-permute-start(bf16[32,8192]{1,0:T(8,128)(2,1)S(1)} %get-tuple-element.705), channel_id=1, source_target_pairs={{32,0},{64,32},{96,64},{128,96},{160,128},{192,160},{224,192},{33,... | collective-permute-start | bytes 1572872 | tf_op jit(solution)/shard_map/while/body/eval_jaxpr/ppermute | solution.py:37
  571.3 42.6 %collective-permute-start.1 = (bf16[32,8192]{1,0:T(8,128)(2,1)S(1)}, bf16[32,8192]{1,0:T(8,128)(2,1)S(1)}, u32[]{:S(2)}, u32[]{:S(2)}) collective-permute-start(bf16[32,8192]{1,0:T(8,128)(2,1)S(1)} %get-tuple-element.705), channel_id=1, source_target_pairs={{32,0},{64,32},{96,64},{128,96},{160,128},{192,160},{224,192},{33,... | collective-permute-start | bytes 1572872 | tf_op jit(solution)/shard_map/while/body/eval_jaxpr/ppermute | solution.py:37
  615.7 6.1 copy-start
  623.9 15.0 %collective-permute-start.1 = (bf16[32,8192]{1,0:T(8,128)(2,1)S(1)}, bf16[32,8192]{1,0:T(8,128)(2,1)S(1)}, u32[]{:S(2)}, u32[]{:S(2)}) collective-permute-start(bf16[32,8192]{1,0:T(8,128)(2,1)S(1)} %get-tuple-element.705), channel_id=1, source_target_pairs={{32,0},{64,32},{96,64},{128,96},{160,128},{192,160},{224,192},{33,... | collective-permute-start | bytes 1572872 | tf_op jit(solution)/shard_map/while/body/eval_jaxpr/ppermute | solution.py:37
  640.7 6.1 copy-start
  648.9 16.4 %collective-permute-start.1 = (bf16[32,8192]{1,0:T(8,128)(2,1)S(1)}, bf16[32,8192]{1,0:T(8,128)(2,1)S(1)}, u32[]{:S(2)}, u32[]{:S(2)}) collective-permute-start(bf16[32,8192]{1,0:T(8,128)(2,1)S(1)} %get-tuple-element.705), channel_id=1, source_target_pairs={{32,0},{64,32},{96,64},{128,96},{160,128},{192,160},{224,192},{33,... | collective-permute-start | bytes 1572872 | tf_op jit(solution)/shard_map/while/body/eval_jaxpr/ppermute | solution.py:37
  667.1 6.1 copy-start
  675.3 19.7 %collective-permute-start.1 = (bf16[32,8192]{1,0:T(8,128)(2,1)S(1)}, bf16[32,8192]{1,0:T(8,128)(2,1)S(1)}, u32[]{:S(2)}, u32[]{:S(2)}) collective-permute-start(bf16[32,8192]{1,0:T(8,128)(2,1)S(1)} %get-tuple-element.705), channel_id=1, source_target_pairs={{32,0},{64,32},{96,64},{128,96},{160,128},{192,160},{224,192},{33,... | collective-permute-start | bytes 1572872 | tf_op jit(solution)/shard_map/while/body/eval_jaxpr/ppermute | solution.py:37
  696.8 6.1 copy-start
  706.1 17.8 %all-to-all-start.2 = ((bf16[32,2,512]{2,1,0:T(2,128)(2,1)}), bf16[32,2,512]{2,1,0:T(2,128)(2,1)S(1)}, u32[]{:S(2)}, u32[]{:S(2)}) async-start(bf16[32,2,512]{2,1,0:T(2,128)(2,1)} %reshape.113), calls=%async_computation.2 | async-start | bytes 131072 | tf_op jit(solution)/shard_map/all_to_all | solution.py:48
  723.9 34.0 %all-to-all-start.1 = ((bf16[32,256,64]{1,2,0:T(8,128)(2,1)}), bf16[32,256,64]{1,2,0:T(8,128)(2,1)S(1)}, u32[]{:S(2)}, u32[]{:S(2)}) async-start(bf16[32,256,64]{1,2,0:T(8,128)(2,1)} %bitcast.80), calls=%async_computation.1 | async-start | bytes 2097152 | tf_op jit(solution)/shard_map/all_to_all | solution.py:48
